TPU v7x, 32 devices: a whole 2x2x4 slice. The times are simulated.
32 devices in a mesh: row: 16 (over z, y, core), col: 2 (over x).
Axes of the slice: x: 2, y: 2, z: 4, core: 2. Of those that a mesh axis runs over, the one named last changes fastest.
Arguments:
- pair_act: bfloat16 [192, 192, 128], P('row', 'col'), may hold values from -6 to 6
- tile_mask: int32 [12, 12], replicated, may hold values 0 or 1
- w_left_gate: bfloat16 [128, 128], replicated, may hold values from -0.5 to 0.5
- w_left: bfloat16 [128, 128], replicated, may hold values from -0.5 to 0.5
- w_right_gate: bfloat16 [128, 128], replicated, may hold values from -0.5 to 0.5
- w_right: bfloat16 [128, 128], replicated, may hold values from -0.5 to 0.5
- w_out_gate: bfloat16 [128, 128], replicated, may hold values from -0.5 to 0.5
- w_out: bfloat16 [128, 128], replicated, may hold values from -0.5 to 0.5
Outputs:
- update: bfloat16 [192, 192, 128], P('row', 'col')
All inputs are finite; a program needn't handle non-finite values.
Results may differ from a plain program's by a relative error of at most 0.0083.
Values may be sent and summed in bfloat16 or wider, within the bound.
A program may use at most 64 MiB of HBM per device.

v0:
```python
import jax
import jax.numpy as jnp
from jax import lax
from jax.sharding import PartitionSpec as P

TILES = 12


def norm_axis(values, axis):
    mean = jnp.mean(values, axis=axis, keepdims=True)
    centred = values - mean
    spread = jnp.mean(centred * centred, axis=axis, keepdims=True)
    return centred * lax.rsqrt(spread + 1e-05)


def local(pair_act, tile_mask, w_left_gate, w_left, w_right_gate, w_right, w_out_gate, w_out):
    rows, cols, width = pair_act.shape
    residues = rows * lax.axis_size("row")
    tile = residues // TILES
    normed = norm_axis(pair_act.astype(jnp.float32), 2).astype(jnp.bfloat16)
    tile_range = lax.iota(jnp.int32, TILES)
    row_ids = (lax.axis_index("row") * rows + lax.iota(jnp.int32, rows)) // tile
    col_ids = (lax.axis_index("col") * cols + lax.iota(jnp.int32, cols)) // tile
    row_hot = (row_ids[:, None] == tile_range[None, :]).astype(jnp.float32)
    col_hot = (col_ids[:, None] == tile_range[None, :]).astype(jnp.float32)
    pair_mask = jnp.dot(
        jnp.dot(row_hot, tile_mask.astype(jnp.float32), preferred_element_type=jnp.float32),
        col_hot.T,
        preferred_element_type=jnp.float32,
    )

    def project(weight):
        return jnp.einsum("ijd,de->eij", normed, weight, preferred_element_type=jnp.float32)

    left = (jax.nn.sigmoid(project(w_left_gate)) * project(w_left) * pair_mask[None]).astype(
        jnp.bfloat16
    )
    right = (jax.nn.sigmoid(project(w_right_gate)) * project(w_right) * pair_mask[None]).astype(
        jnp.bfloat16
    )
    left_rows, right_rows = (
        lax.all_to_all(left, "row", split_axis=0, concat_axis=1, tiled=True),
        lax.all_to_all(right, "row", split_axis=0, concat_axis=1, tiled=True),
    )
    right_block = lax.all_to_all(right_rows, "col", split_axis=1, concat_axis=2, tiled=True)
    triangle = jnp.einsum(
        "cik,cjk->jci",
        lax.all_gather(left_rows, "col", axis=2, tiled=True),
        right_block,
        preferred_element_type=jnp.float32,
    )
    triangle = triangle.astype(jnp.bfloat16)
    owned = lax.all_to_all(triangle, "row", split_axis=2, concat_axis=1, tiled=True)
    scaled = norm_axis(owned.astype(jnp.float32), 1).astype(jnp.bfloat16)
    projected = jnp.einsum("jci,ce->ije", scaled, w_out, preferred_element_type=jnp.float32)
    gate = jax.nn.sigmoid(
        jnp.einsum("ijd,de->ije", normed, w_out_gate, preferred_element_type=jnp.float32)
    )
    return (gate * projected).astype(jnp.bfloat16)


def solution(mesh):
    return jax.shard_map(
        local,
        mesh=mesh,
        in_specs=(P("row", "col", None), P(), P(), P(), P(), P(), P(), P()),
        out_specs=P("row", "col", None),
        check_vma=False,
    )
```

profile of v0, /device:TPU:0, one launch (start us, length us, event | category | flops | bytes accessed | tf_op | source)
XLA Modules:
  0.0 84.8 jit_solution(9804419726071187752)
XLA Ops:
  0.0 1.2 %convert_reduce_fusion = f32[12,96]{1,0:T(8,128)S(1)} fusion(bf16[12,96,128]{2,1,0:T(8,128)(2,1)} %param.8), kind=kLoop, calls=%fused_computation.34 | loop fusion | flops 293760 | bytes 299520 | tf_op jit(solution)/shard_map/reduce_sum | solution.py:10
  1.2 0.5 fusion.26
  1.7 0.8 fusion.8
  2.8 0.5 copy-done.2
  3.3 0.5 fusion.17
  3.8 1.2 %copy.22 = bf16[128,12,96]{2,1,0:T(8,128)(2,1)} copy(bf16[128,12,96]{0,2,1:T(8,128)(2,1)S(1)} %fusion.17) | data formatting | bytes 589824 | tf_op jit(solution)/shard_map/convert_element_type | solution.py:38
  5.0 7.5 %all-to-all-start = ((bf16[128,12,96]{2,1,0:T(8,128)(2,1)}), bf16[128,12,96]{2,1,0:T(8,128)(2,1)S(1)}, u32[]{:S(2)}, u32[]{:S(2)}) async-start(bf16[128,12,96]{2,1,0:T(8,128)(2,1)} %copy.22), calls=%async_computation | async-start | bytes 1048576 | tf_op jit(solution)/shard_map/all_to_all | solution.py:43
  12.6 0.8 fusion.5
  13.4 0.5 fusion.16
  13.9 1.2 %copy.27 = bf16[128,12,96]{2,1,0:T(8,128)(2,1)} copy(bf16[128,12,96]{0,2,1:T(8,128)(2,1)S(1)} %fusion.16) | data formatting | bytes 589824 | tf_op jit(solution)/shard_map/convert_element_type | solution.py:35
  15.1 11.7 %all-to-all-done = bf16[128,12,96]{2,1,0:T(8,128)(2,1)S(1)} async-done(((bf16[128,12,96]{2,1,0:T(8,128)(2,1)}), bf16[128,12,96]{2,1,0:T(8,128)(2,1)S(1)}, u32[]{:S(2)}, u32[]{:S(2)}) %all-to-all-start) | async-done | bytes 294944 | tf_op jit(solution)/shard_map/all_to_all | solution.py:43
  26.8 4.2 %all-to-all-start.2 = ((bf16[128,12,96]{2,1,0:T(8,128)(2,1)}), bf16[128,12,96]{2,1,0:T(8,128)(2,1)S(1)}, u32[]{:S(2)}, u32[]{:S(2)}) async-start(bf16[128,12,96]{2,1,0:T(8,128)(2,1)} %copy.27), calls=%async_computation.2 | async-start | bytes 1048576 | tf_op jit(solution)/shard_map/all_to_all | solution.py:42
  31.0 0.8 copy.24
  31.9 13.4 %all-to-all-done.2 = bf16[128,12,96]{2,1,0:T(8,128)(2,1)S(1)} async-done(((bf16[128,12,96]{2,1,0:T(8,128)(2,1)}), bf16[128,12,96]{2,1,0:T(8,128)(2,1)S(1)}, u32[]{:S(2)}, u32[]{:S(2)}) %all-to-all-start.2) | async-done | bytes 294944 | tf_op jit(solution)/shard_map/all_to_all | solution.py:42
  45.3 3.5 %all-to-all-start.1 = ((bf16[8,192,96]{2,0,1:T(8,128)(2,1)}), bf16[8,192,96]{2,0,1:T(8,128)(2,1)S(1)}, u32[]{:S(2)}, u32[]{:S(2)}) async-start(bf16[8,192,96]{2,0,1:T(8,128)(2,1)} %bitcast.7), calls=%async_computation.1 | async-start | bytes 786432 | tf_op jit(solution)/shard_map/all_to_all | solution.py:45
  48.9 0.4 copy.30
  49.3 15.0 %all_gather.3 = bf16[8,192,192]{1,0,2:T(8,128)(2,1)S(1)} all-gather(bf16[8,192,96]{1,0,2:T(8,128)(2,1)S(1)} %copy.30), channel_id=1, replica_groups=mesh['row'=16,'col'=2] {'col'}, dimensions={2}, use_global_device_ids=true | all-gather | bytes 884736 | tf_op jit(solution)/shard_map/all_gather | solution.py:48
  64.3 0.4 copy.26
  65.3 1.0 %copy.32 = bf16[96,8,192]{0,1,2:T(8,128)(2,1)} copy(bf16[96,8,192]{2,0,1:T(8,128)(2,1)S(1)} %fusion.15) | data formatting | bytes 589824 | tf_op jit(solution)/shard_map/convert_element_type | solution.py:52
  66.2 4.5 %all-to-all-start.3 = ((bf16[96,8,192]{0,1,2:T(8,128)(2,1)}), bf16[96,8,192]{0,1,2:T(8,128)(2,1)S(1)}, u32[]{:S(2)}, u32[]{:S(2)}) async-start(bf16[96,8,192]{0,1,2:T(8,128)(2,1)} %copy.32), calls=%async_computation.3 | async-start | bytes 786432 | tf_op jit(solution)/shard_map/all_to_all | solution.py:53
  70.8 0.8 fusion.11
  71.6 11.4 %all-to-all-done.3 = bf16[96,8,192]{0,1,2:T(8,128)(2,1)S(1)} async-done(((bf16[96,8,192]{0,1,2:T(8,128)(2,1)}), bf16[96,8,192]{0,1,2:T(8,128)(2,1)S(1)}, u32[]{:S(2)}, u32[]{:S(2)}) %all-to-all-start.3) | async-done | bytes 294944 | tf_op jit(solution)/shard_map/all_to_all | solution.py:53
  83.2 0.6 copy-done.4
  83.8 1.0 %fusion.14 = bf16[12,96,128]{2,1,0:T(8,128)(2,1)} fusion(f32[12,96,128]{2,1,0:T(8,128)S(1)} %fusion.11, f32[96,12]{0,1:T(8,128)S(1)} %add_rsqrt_fusion, f32[96,12]{0,1:T(8,128)S(1)} %broadcast_multiply_fusion, bf16[128,128]{1,0:T(8,128)(2,1)S(1)} %copy-done.4, bf16[96,8,16,12]{0,1,3,2:T(8,128)(2,1)S(1)} %bitcast.61), kind=kOutput, calls=%fused_computation.21 | convolution fusion | flops 38633472 | bytes 1221632 | tf_op jit(solution)/shard_map/jci,ce->ije/dot_general | solution.py:55
  (27 shorter events, 1.2 us)
Async XLA Ops:
  0.0 1.7 %copy-start = (bf16[128,128]{1,0:T(8,128)(2,1)S(1)}, bf16[128,128]{1,0:T(8,128)(2,1)}, u32[]{:S(2)}) copy-start(bf16[128,128]{1,0:T(8,128)(2,1)} %param.12) | copy-start | bytes 98308
  0.0 1.2 %copy-start.1 = (bf16[12,96,128]{2,1,0:T(8,128)(2,1)S(1)}, bf16[12,96,128]{2,1,0:T(8,128)(2,1)}, u32[]{:S(2)}) copy-start(bf16[12,96,128]{2,1,0:T(8,128)(2,1)} %param.8) | copy-start | bytes 884740
  1.7 0.8 copy-start.7
  2.5 0.8 copy-start.2
  5.0 7.6 %copy-start.5 = (bf16[128,128]{1,0:T(8,128)(2,1)S(1)}, bf16[128,128]{1,0:T(8,128)(2,1)}, u32[]{:S(2)}) copy-start(bf16[128,128]{1,0:T(8,128)(2,1)} %param.10) | copy-start | bytes 98308
  5.0 21.8 %all-to-all-start = ((bf16[128,12,96]{2,1,0:T(8,128)(2,1)}), bf16[128,12,96]{2,1,0:T(8,128)(2,1)S(1)}, u32[]{:S(2)}, u32[]{:S(2)}) async-start(bf16[128,12,96]{2,1,0:T(8,128)(2,1)} %copy.22), calls=%async_computation | async-start | bytes 1048576 | tf_op jit(solution)/shard_map/all_to_all | solution.py:43
  12.6 0.8 copy-start.3
  26.8 18.4 %all-to-all-start.2 = ((bf16[128,12,96]{2,1,0:T(8,128)(2,1)}), bf16[128,12,96]{2,1,0:T(8,128)(2,1)S(1)}, u32[]{:S(2)}, u32[]{:S(2)}) async-start(bf16[128,12,96]{2,1,0:T(8,128)(2,1)} %copy.27), calls=%async_computation.2 | async-start | bytes 1048576 | tf_op jit(solution)/shard_map/all_to_all | solution.py:42
  45.3 19.0 %all-to-all-start.1 = ((bf16[8,192,96]{2,0,1:T(8,128)(2,1)}), bf16[8,192,96]{2,0,1:T(8,128)(2,1)S(1)}, u32[]{:S(2)}, u32[]{:S(2)}) async-start(bf16[8,192,96]{2,0,1:T(8,128)(2,1)} %bitcast.7), calls=%async_computation.1 | async-start | bytes 786432 | tf_op jit(solution)/shard_map/all_to_all | solution.py:45
  66.2 4.6 %copy-start.6 = (bf16[128,128]{1,0:T(8,128)(2,1)S(1)}, bf16[128,128]{1,0:T(8,128)(2,1)}, u32[]{:S(2)}) copy-start(bf16[128,128]{1,0:T(8,128)(2,1)} %param.14) | copy-start | bytes 98308
  66.2 16.7 %all-to-all-start.3 = ((bf16[96,8,192]{0,1,2:T(8,128)(2,1)}), bf16[96,8,192]{0,1,2:T(8,128)(2,1)S(1)}, u32[]{:S(2)}, u32[]{:S(2)}) async-start(bf16[96,8,192]{0,1,2:T(8,128)(2,1)} %copy.32), calls=%async_computation.3 | async-start | bytes 786432 | tf_op jit(solution)/shard_map/all_to_all | solution.py:53
  83.1 0.8 copy-start.4
where the time goes:
time: 85.6 us; the launch traced here: 84.8 us
  waiting for transfers between devices  36.5 us (43%)
  starting transfers between devices  19.7 us (23%)
  blocking collectives  15 us (18%)
  local copies, waits for them, and re-layouts  6.45 us (8%)
  matrix products  4.94 us (6%)
  other arithmetic  1.92 us (2%)
    all_gather x1, blocking collectives, local(): lax.all_gather(left_rows, 'col', axis=2, tiled=True)  15 us
    all_to_all x1, waiting for transfers between devices, local(): lax.all_to_all(left, 'row', split_axis=0, concat_axis=1, tiled=True)  13.4 us
    all_to_all x1, waiting for transfers between devices, local(): lax.all_to_all(right, 'row', split_axis=0, concat_axis=1, tiled=True)  11.7 us
    all_to_all x1, waiting for transfers between devices, local(): lax.all_to_all(triangle, 'row', split_axis=2, concat_axis=1, tiled=True)  11.4 us
    all_to_all x1, starting transfers between devices, local(): lax.all_to_all(right, 'row', split_axis=0, concat_axis=1, tiled=True)  7.55 us
    all_to_all x1, starting transfers between devices, local(): lax.all_to_all(triangle, 'row', split_axis=2, concat_axis=1, tiled=True)  4.54 us
    all_to_all x1, starting transfers between devices, local(): lax.all_to_all(left, 'row', split_axis=0, concat_axis=1, tiled=True)  4.16 us
    all_to_all x1, starting transfers between devices, local(): lax.all_to_all(right_rows, 'col', split_axis=1, concat_axis=2, tiled=True)  3.47 us
  transfers between devices with their start and end apart: 4, of which 3 were waited for; matrix products, arithmetic and copies ran while one was open for 5% of the time, Pallas kernels for 0%

commit v1 on v0

v1 whole, which is shorter than its diff:
```python
import functools

import jax
import jax.numpy as jnp
from jax import lax
from jax.experimental import pallas as pl
from jax.experimental.pallas import tpu as pltpu
from jax.sharding import PartitionSpec as P

TILES = 12
GROUP = 8
MESH = pl.DeviceIdType.MESH


def norm_axis(values, axis):
    mean = jnp.mean(values, axis=axis, keepdims=True)
    centred = values - mean
    spread = jnp.mean(centred * centred, axis=axis, keepdims=True)
    return centred * lax.rsqrt(spread + 1e-05)


def place(flat, col_size):
    return (flat // col_size, flat % col_size)


def greet(flat, first, count, col_size):
    barrier = pltpu.get_barrier_semaphore()

    def signal(step, _):
        other = first + (flat - first + step) % count
        pl.semaphore_signal(barrier, inc=1, device_id=place(other, col_size), device_id_type=MESH)
        return 0

    lax.fori_loop(1, count, signal, 0)
    pl.semaphore_wait(barrier, count - 1)


def spread_kernel(
    sizes, left, right, left_all, right_all, own_sem, left_send, left_recv, right_send, right_recv
):
    row_size, col_size, groups = sizes
    devices = row_size * col_size
    flat = lax.axis_index("row") * col_size + lax.axis_index("col")
    member = flat % groups
    first = flat - member

    def chunk(source, group):
        return source.at[group]

    own_left = pltpu.make_async_copy(chunk(left, member), left_all.at[member], own_sem.at[0])
    own_right = pltpu.make_async_copy(chunk(right, member), right_all.at[flat], own_sem.at[1])
    own_left.start()
    own_right.start()
    greet(flat, 0, devices, col_size)

    def right_copy(step):
        to = (flat + step) % devices
        return pltpu.make_async_remote_copy(
            src_ref=chunk(right, to % groups),
            dst_ref=right_all.at[flat],
            send_sem=right_send.at[step],
            recv_sem=right_recv.at[step],
            device_id=place(to, col_size),
            device_id_type=MESH,
        )

    def left_copy(step):
        to = (member + step) % groups
        return pltpu.make_async_remote_copy(
            src_ref=chunk(left, to),
            dst_ref=left_all.at[member],
            send_sem=left_send.at[step],
            recv_sem=left_recv.at[step],
            device_id=place(first + to, col_size),
            device_id_type=MESH,
        )

    def start_right(step, _):
        right_copy(step).start()
        return 0

    def start_left(step, _):
        left_copy(step).start()
        return 0

    def wait_right(step, _):
        right_copy(step).wait()
        return 0

    def wait_left(step, _):
        left_copy(step).wait()
        return 0

    lax.fori_loop(1, devices, start_right, 0)
    lax.fori_loop(1, groups, start_left, 0)
    own_left.wait()
    own_right.wait()
    lax.fori_loop(1, groups, wait_left, 0)
    lax.fori_loop(1, devices, wait_right, 0)


def return_kernel(sizes, triangle, owned, own_sem, send, recv):
    row_size, col_size, groups = sizes
    flat = lax.axis_index("row") * col_size + lax.axis_index("col")
    member = flat % groups
    first = flat - member
    own = pltpu.make_async_copy(triangle.at[member], owned.at[member], own_sem)
    own.start()
    greet(flat, first, groups, col_size)

    def copy(step):
        to = (member + step) % groups
        return pltpu.make_async_remote_copy(
            src_ref=triangle.at[to],
            dst_ref=owned.at[member],
            send_sem=send.at[step],
            recv_sem=recv.at[step],
            device_id=place(first + to, col_size),
            device_id_type=MESH,
        )

    def start(step, _):
        copy(step).start()
        return 0

    def wait(step, _):
        copy(step).wait()
        return 0

    lax.fori_loop(1, groups, start, 0)
    own.wait()
    lax.fori_loop(1, groups, wait, 0)


def local(
    sizes, pair_act, tile_mask, w_left_gate, w_left, w_right_gate, w_right, w_out_gate, w_out
):
    row_size, col_size, groups = sizes
    devices = row_size * col_size
    block_rows = groups // col_size
    rows, cols, width = pair_act.shape
    residues = rows * row_size
    tile = residues // TILES
    normed = norm_axis(pair_act.astype(jnp.float32), 2).astype(jnp.bfloat16)
    tile_range = lax.iota(jnp.int32, TILES)
    row_ids = (lax.axis_index("row") * rows + lax.iota(jnp.int32, rows)) // tile
    col_ids = (lax.axis_index("col") * cols + lax.iota(jnp.int32, cols)) // tile
    row_hot = (row_ids[:, None] == tile_range[None, :]).astype(jnp.float32)
    col_hot = (col_ids[:, None] == tile_range[None, :]).astype(jnp.float32)
    pair_mask = jnp.dot(
        jnp.dot(row_hot, tile_mask.astype(jnp.float32), preferred_element_type=jnp.float32),
        col_hot.T,
        preferred_element_type=jnp.float32,
    )
    pairs = rows * cols
    flat_normed = normed.reshape(pairs, width)
    flat_mask = pair_mask.reshape(1, pairs)

    def project(weight):
        return jnp.einsum("pd,de->ep", flat_normed, weight, preferred_element_type=jnp.float32)

    def factor(gate, value):
        out = jax.nn.sigmoid(project(gate)) * project(value) * flat_mask
        return out.astype(jnp.bfloat16).reshape(groups, GROUP, pairs)

    left = factor(w_left_gate, w_left)
    right = factor(w_right_gate, w_right)
    anywhere = pl.BlockSpec(memory_space=pl.ANY)
    left_all, right_all = pl.pallas_call(
        functools.partial(spread_kernel, sizes),
        out_shape=(
            jax.ShapeDtypeStruct((groups, GROUP, pairs), jnp.bfloat16),
            jax.ShapeDtypeStruct((devices, GROUP, pairs), jnp.bfloat16),
        ),
        in_specs=[anywhere] * 2,
        out_specs=(anywhere, anywhere),
        scratch_shapes=[
            pltpu.SemaphoreType.DMA((2,)),
            pltpu.SemaphoreType.DMA((groups,)),
            pltpu.SemaphoreType.DMA((groups,)),
            pltpu.SemaphoreType.DMA((devices,)),
            pltpu.SemaphoreType.DMA((devices,)),
        ],
        compiler_params=pltpu.CompilerParams(collective_id=0, has_side_effects=True),
    )(left, right)
    left_rows = (
        left_all.reshape(block_rows, col_size, GROUP, rows, cols)
        .transpose(2, 0, 3, 1, 4)
        .reshape(GROUP, block_rows * rows, residues)
    )
    right_rows = (
        right_all.reshape(row_size, col_size, GROUP, rows, cols)
        .transpose(2, 0, 3, 1, 4)
        .reshape(GROUP, residues, residues)
    )
    triangle = jnp.einsum(
        "cik,cjk->cij", left_rows, right_rows, preferred_element_type=jnp.float32
    ).astype(jnp.bfloat16)
    triangle = (
        triangle.reshape(GROUP, block_rows, rows, col_size, cols)
        .transpose(1, 3, 0, 2, 4)
        .reshape(groups, GROUP, pairs)
    )
    owned = pl.pallas_call(
        functools.partial(return_kernel, sizes),
        out_shape=jax.ShapeDtypeStruct((groups, GROUP, pairs), jnp.bfloat16),
        in_specs=[anywhere],
        out_specs=anywhere,
        scratch_shapes=[
            pltpu.SemaphoreType.DMA,
            pltpu.SemaphoreType.DMA((groups,)),
            pltpu.SemaphoreType.DMA((groups,)),
        ],
        compiler_params=pltpu.CompilerParams(collective_id=1, has_side_effects=True),
    )(triangle)
    owned = owned.reshape(width, pairs)
    scaled = norm_axis(owned.astype(jnp.float32), 0).astype(jnp.bfloat16)
    projected = jnp.einsum("cp,ce->pe", scaled, w_out, preferred_element_type=jnp.float32)
    gate = jax.nn.sigmoid(
        jnp.einsum("pd,de->pe", flat_normed, w_out_gate, preferred_element_type=jnp.float32)
    )
    return (gate * projected).astype(jnp.bfloat16).reshape(rows, cols, width)


def solution(mesh):
    def whole(pair_act, tile_mask, *weights):
        groups = pair_act.shape[2] // GROUP
        sizes = (mesh.shape["row"], mesh.shape["col"], groups)
        return jax.shard_map(
            functools.partial(local, sizes),
            mesh=mesh,
            in_specs=(P("row", "col", None), P(), P(), P(), P(), P(), P(), P()),
            out_specs=P("row", "col", None),
            check_vma=False,
        )(pair_act, tile_mask, *weights)

    return whole
```

time: 85.6 us -> 50.3 us (0.59)
  waiting for transfers between devices: 36.5 us -> 0 us
  Pallas kernels: 0 us -> 31.5 us
  starting transfers between devices: 19.7 us -> 0 us
  blocking collectives: 15 us -> 0 us
  local copies, waits for them, and re-layouts: 6.45 us -> 11.8 us
  matrix products: 4.94 us -> 3.08 us
  other arithmetic: 1.92 us -> 3.26 us
    all_to_all x4 -> x0, waiting for transfers between devices: 36.5 us -> none  [the longest x1 13.4 us: local(): lax.all_to_all(left, 'row', split_axis=0, concat_axis=1, tiled=True)]
    pallas_call x0 -> x2, Pallas kernels: none -> 31.5 us  [the longest x1 21.5 us: local(): pl.pallas_call(functools.partial(spread_kernel, sizes), out_shape=(jax.Sh...]
    all_to_all x4 -> x0, starting transfers between devices: 19.7 us -> none  [the longest x1 7.55 us: local(): lax.all_to_all(right, 'row', split_axis=0, concat_axis=1, tiled=True)]
    all_gather x1 -> x0, blocking collectives: 15 us -> none  [local(): lax.all_gather(left_rows, 'col', axis=2, tiled=True)]
    reshape x0 -> x7, local copies, waits for them, and re-layouts: none -> 5.18 us  [the longest x1 2.43 us: local(): right_all.reshape(row_size, col_size, GROUP, rows, cols)]
    unnamed x16 -> x20, local copies, waits for them, and re-layouts: 1.08 us -> 3.09 us
    all_to_all x5 -> x0, local copies, waits for them, and re-layouts: 2 us -> none  [the longest x1 0.85 us: local(): lax.all_to_all(right, 'row', split_axis=0, concat_axis=1, tiled=True)]
    dot_general x7, matrix products: 4.65 us -> 2.79 us  [the longest x4 1.1 us: project(): jnp.einsum('pd,de->ep', flat_normed, weight, preferred_element_type=jnp.f...]
  transfers between devices with their start and end apart: 4 -> 0, of which waited for: 3 -> 0; matrix products, arithmetic and copies ran while one was open for 5% -> 0% of each run, Pallas kernels for 0% -> 0%
where the time goes in v1:
time: 50.3 us; the launch traced here: 49.8 us
  Pallas kernels  31.5 us (63%)
  local copies, waits for them, and re-layouts  11.8 us (23%)
  other arithmetic  3.26 us (6%)
  matrix products  3.08 us (6%)
    pallas_call x1, Pallas kernels, local(): pl.pallas_call(functools.partial(spread_kernel, sizes), out_shape=(jax.Sh...  21.5 us
    pallas_call x1, Pallas kernels, local(): pl.pallas_call(functools.partial(return_kernel, sizes), out_shape=jax.Sha...  10 us
    unnamed x20, local copies, waits for them, and re-layouts  3.09 us
    reshape x1, local copies, waits for them, and re-layouts, local(): right_all.reshape(row_size, col_size, GROUP, rows, cols)  2.43 us
    reduce_sum x2, other arithmetic, norm_axis(): mean = jnp.mean(values, axis=axis, keepdims=True)  2.29 us
    convert_element_type x2, local copies, waits for them, and re-layouts, factor(): return out.astype(jnp.bfloat16).reshape(groups, GROUP, pairs)  1.79 us
    transpose x1, local copies, waits for them, and re-layouts, local(): right_rows = right_all.reshape(row_size, col_size, GROUP, rows, cols).tra...  1.22 us
    dot_general x4, matrix products, project(): jnp.einsum('pd,de->ep', flat_normed, weight, preferred_element_type=jnp.f...  1.1 us

profile of v1, /device:TPU:0, one launch (start us, length us, event | category | flops | bytes accessed | tf_op | source)
XLA Modules:
  0.0 49.8 jit_solution(5813699214639899910)
XLA Ops:
  0.0 1.2 %convert_reduce_fusion.1 = f32[12,96]{1,0:T(8,128)S(1)} fusion(bf16[12,96,128]{2,1,0:T(8,128)(2,1)} %param.8), kind=kLoop, calls=%fused_computation.29 | loop fusion | flops 293760 | bytes 299520 | tf_op jit(solution)/shard_map/reduce_sum | solution.py:16
  1.2 0.5 fusion.21
  1.7 0.4 fusion.22
  2.1 0.3 fusion.7
  2.5 0.7 %copy-done.9 = s32[12,12]{1,0:T(8,128)S(1)} copy-done((s32[12,12]{1,0:T(8,128)S(1)}, s32[12,12]{1,0:T(8,128)}, u32[]{:S(2)}) %copy-start.9) | copy-done | bytes 600
  3.5 0.4 copy-done.4
  4.2 0.9 %copy.27 = bf16[128,1152]{1,0:T(8,128)(2,1)} copy(bf16[128,1152]{0,1:T(8,128)(2,1)S(1)} %fusion.15) | data formatting | bytes 589824 | tf_op jit(solution)/shard_map/convert_element_type | solution.py:164
  5.1 0.3 fusion.4
  5.4 0.4 copy-done.5
  6.1 0.9 %copy.30 = bf16[128,1152]{1,0:T(8,128)(2,1)} copy(bf16[128,1152]{0,1:T(8,128)(2,1)S(1)} %fusion.14) | data formatting | bytes 589824 | tf_op jit(solution)/shard_map/convert_element_type | solution.py:164
  6.9 21.5 %shard_map.82 = (bf16[16,8,1152]{2,1,0:T(8,128)(2,1)}, bf16[32,8,1152]{2,1,0:T(8,128)(2,1)}) custom-call(bf16[16,8,1152]{2,1,0:T(8,128)(2,1)} %bitcast.43, bf16[16,8,1152]{2,1,0:T(8,128)(2,1)} %bitcast.44), custom_call_target="tpu_custom_call" | custom-call | tf_op jit(solution)/shard_map/pallas_call | solution.py:169
  28.4 2.4 %reshape.107 = bf16[16,2,8,12,96]{4,3,2,1,0:T(8,128)(2,1)S(1)} reshape(bf16[32,8,1152]{2,1,0:T(8,128)(2,1)} %get-tuple-element.8) | data formatting | bytes 1179648 | tf_op jit(solution)/shard_map/reshape | solution.py:192
  30.8 1.2 %copy.32 = bf16[8,16,12,2,96]{4,3,2,1,0:T(2,128)(2,1)S(1)} copy(bf16[8,16,12,2,96]{4,2,0,3,1:T(8,128)(2,1)S(1)} %bitcast.35) | data formatting | bytes 1179648 | tf_op jit(solution)/shard_map/transpose | solution.py:193
  32.1 0.4 reshape.108
  32.5 0.5 copy-done.3
  33.0 0.7 %reshape.105 = bf16[8,2,8,12,96]{4,3,2,1,0:T(8,128)(2,1)S(1)} reshape(bf16[16,8,1152]{2,1,0:T(8,128)(2,1)S(1)} %copy-done.3) | data formatting | bytes 589824 | tf_op jit(solution)/shard_map/reshape | solution.py:187
  33.7 0.4 copy.31
  34.3 0.4 convolution_convert_fusion
  35.1 1.1 %reshape.110.triangle = bf16[16,8,1152]{2,1,0:T(8,128)(2,1)} reshape(bf16[8,2,8,12,96]{4,3,2,1,0:T(8,128)(2,1)S(1)} %bitcast.42) | data formatting | bytes 589824 | tf_op jit(solution)/shard_map/reshape | solution.py:202
  36.2 10.0 %shard_map.83 = bf16[16,8,1152]{2,1,0:T(8,128)(2,1)} custom-call(bf16[16,8,1152]{2,1,0:T(8,128)(2,1)} %reshape.110.triangle), custom_call_target="tpu_custom_call" | custom-call | tf_op jit(solution)/shard_map/pallas_call | solution.py:204
  46.2 1.1 %convert_reduce_fusion = f32[1152]{0:T(1024)S(1)} fusion(bf16[16,8,1152]{2,1,0:T(8,128)(2,1)} %shard_map.83), kind=kLoop, calls=%fused_computation.26 | loop fusion | flops 293760 | bytes 299520 | tf_op jit(solution)/shard_map/reduce_sum | solution.py:16
  47.4 0.6 %copy-done.8 = bf16[128,128]{1,0:T(8,128)(2,1)S(1)} copy-done((bf16[128,128]{1,0:T(8,128)(2,1)S(1)}, bf16[128,128]{1,0:T(8,128)(2,1)}, u32[]{:S(2)}) %copy-start.8) | copy-done | bytes 32792
  48.4 0.4 copy-done.6
  48.8 1.0 %fusion.13 = bf16[1152,128]{1,0:T(8,128)(2,1)} fusion(f32[1152,128]{1,0:T(8,128)S(1)} %fusion.10, bf16[128,128]{1,0:T(8,128)(2,1)S(1)} %copy-done.6, bf16[16,8,1152]{2,1,0:T(8,128)(2,1)S(1)} %copy-done.1, f32[1152]{0:T(1024)S(1)} %add_rsqrt_fusion, f32[1152]{0:T(1024)S(1)} %broadcast_multiply_fusion), kind=kOutput, calls=%fused_computation.19 | convolution fusion | flops 38633472 | bytes 1221632 | tf_op jit(solution)/shard_map/cp,ce->pe/dot_general | solution.py:218
  (29 shorter events, 1.9 us)
Async XLA Ops:
  0.0 2.1 %copy-start = (bf16[128,128]{1,0:T(8,128)(2,1)S(1)}, bf16[128,128]{1,0:T(8,128)(2,1)}, u32[]{:S(2)}) copy-start(bf16[128,128]{1,0:T(8,128)(2,1)} %param.10) | copy-start | bytes 98308
  0.0 1.2 %copy-start.2 = (bf16[12,96,128]{2,1,0:T(8,128)(2,1)S(1)}, bf16[12,96,128]{2,1,0:T(8,128)(2,1)}, u32[]{:S(2)}) copy-start(bf16[12,96,128]{2,1,0:T(8,128)(2,1)} %param.8) | copy-start | bytes 884740
  2.4 0.7 %copy-start.9 = (s32[12,12]{1,0:T(8,128)S(1)}, s32[12,12]{1,0:T(8,128)}, u32[]{:S(2)}) copy-start(s32[12,12]{1,0:T(8,128)} %param.9) | copy-start | bytes 1732
  3.1 0.8 %copy-start.4 = (bf16[128,128]{1,0:T(8,128)(2,1)S(1)}, bf16[128,128]{1,0:T(8,128)(2,1)}, u32[]{:S(2)}) copy-start(bf16[128,128]{1,0:T(8,128)(2,1)} %param.11) | copy-start | bytes 98308
  4.1 0.9 %copy-start.7 = (bf16[128,128]{1,0:T(8,128)(2,1)S(1)}, bf16[128,128]{1,0:T(8,128)(2,1)}, u32[]{:S(2)}) copy-start(bf16[128,128]{1,0:T(8,128)(2,1)} %param.12) | copy-start | bytes 98308
  5.0 0.8 %copy-start.5 = (bf16[128,128]{1,0:T(8,128)(2,1)S(1)}, bf16[128,128]{1,0:T(8,128)(2,1)}, u32[]{:S(2)}) copy-start(bf16[128,128]{1,0:T(8,128)(2,1)} %param.13) | copy-start | bytes 98308
  32.1 1.0 %copy-start.3 = (bf16[16,8,1152]{2,1,0:T(8,128)(2,1)S(1)}, bf16[16,8,1152]{2,1,0:T(8,128)(2,1)}, u32[]{:S(2)}) copy-start(bf16[16,8,1152]{2,1,0:T(8,128)(2,1)} %get-tuple-element.7) | copy-start | bytes 884740
  46.2 1.1 %copy-start.1 = (bf16[16,8,1152]{2,1,0:T(8,128)(2,1)S(1)}, bf16[16,8,1152]{2,1,0:T(8,128)(2,1)}, u32[]{:S(2)}) copy-start(bf16[16,8,1152]{2,1,0:T(8,128)(2,1)} %shard_map.83) | copy-start | bytes 884740
  47.3 0.8 %copy-start.8 = (bf16[128,128]{1,0:T(8,128)(2,1)S(1)}, bf16[128,128]{1,0:T(8,128)(2,1)}, u32[]{:S(2)}) copy-start(bf16[128,128]{1,0:T(8,128)(2,1)} %param.14) | copy-start | bytes 98308
  48.0 0.8 %copy-start.6 = (bf16[128,128]{1,0:T(8,128)(2,1)S(1)}, bf16[128,128]{1,0:T(8,128)(2,1)}, u32[]{:S(2)}) copy-start(bf16[128,128]{1,0:T(8,128)(2,1)} %param.15) | copy-start | bytes 98308

commit v2 on v1

--- a/solution.py
+++ b/solution.py
@@ -222,12 +222,268 @@
     return (gate * projected).astype(jnp.bfloat16).reshape(rows, cols, width)
 
 
+LANES = 128
+
+
+def fused_kernel(
+    sizes, shape, pair, tiles, w_left_gate, w_left, w_right_gate, w_right, w_out_gate, w_out, out,
+    normed, gate, left, right, left_all, right_all, left_mat, right_mat, product, triangle, owned,
+    left_send, left_recv, right_send, right_recv, back_send, back_recv,
+):
+    row_size, col_size, groups = sizes
+    rows, cols, width = shape
+    devices = row_size * col_size
+    blocks = devices // groups
+    block_rows = groups // col_size
+    pairs = rows * cols
+    tile = rows * row_size // TILES
+    row, col = lax.axis_index("row"), lax.axis_index("col")
+    flat = row * col_size + col
+    member = flat % groups
+    block = flat // groups
+    first = block * groups
+
+    barrier = pltpu.get_barrier_semaphore()
+
+    def signal(step, _):
+        pl.semaphore_signal(
+            barrier, inc=1, device_id=place((flat + step) % devices, col_size), device_id_type=MESH
+        )
+        return 0
+
+    lax.fori_loop(1, devices, signal, 0)
+
+    values = pair[...].astype(jnp.float32)
+    normed[...] = norm_axis(values, 1).astype(jnp.bfloat16)
+
+    spot = lax.broadcasted_iota(jnp.int32, (1, pairs), 1)
+    within = spot
+    for line in range(1, rows):
+        within = jnp.where(spot >= line * cols, spot - line * cols, within)
+    tile_ids = lax.broadcasted_iota(jnp.int32, (TILES, pairs), 0)
+    row_low = (tile_ids * tile - row * rows) * cols
+    row_hot = ((spot >= row_low) & (spot < row_low + tile * cols)).astype(jnp.float32)
+    col_low = tile_ids * tile - col * cols
+    col_hot = ((within >= col_low) & (within < col_low + tile)).astype(jnp.float32)
+    picked = jnp.dot(tiles[...].astype(jnp.float32).T, row_hot, preferred_element_type=jnp.float32)
+    mask = jnp.sum(picked * col_hot, axis=0, keepdims=True)
+
+    def project(weight):
+        turned = weight[...].astype(jnp.float32).T.astype(jnp.bfloat16)
+        return lax.dot_general(
+            turned, normed[...], (((1,), (1,)), ((), ())), preferred_element_type=jnp.float32
+        )
+
+    def factor(gate_weight, weight, target):
+        made = jax.nn.sigmoid(project(gate_weight)) * project(weight) * mask
+        for group in range(groups):
+            target[group] = made[group * GROUP : (group + 1) * GROUP].astype(jnp.bfloat16)
+
+    def right_copy(ahead, step):
+        to = (member + step) % groups
+        return pltpu.make_async_remote_copy(
+            src_ref=right.at[to],
+            dst_ref=right_all.at[flat],
+            send_sem=right_send.at[ahead * groups + step],
+            recv_sem=right_recv.at[ahead * groups + step],
+            device_id=place((block + ahead) % blocks * groups + to, col_size),
+            device_id_type=MESH,
+        )
+
+    def member_copy(source, target, send, recv, step):
+        to = (member + step) % groups
+        return pltpu.make_async_remote_copy(
+            src_ref=source.at[to],
+            dst_ref=target.at[member],
+            send_sem=send.at[step],
+            recv_sem=recv.at[step],
+            device_id=place(first + to, col_size),
+            device_id_type=MESH,
+        )
+
+    def left_copy(step):
+        return member_copy(left, left_all, left_send, left_recv, step)
+
+    def back_copy(step):
+        return member_copy(triangle, owned, back_send, back_recv, step)
+
+    def each(start, stop, do):
+        def body(step, _):
+            do(step)
+            return 0
+
+        lax.fori_loop(start, stop, body, 0)
+
+    factor(w_right_gate, w_right, right)
+    pl.semaphore_wait(barrier, devices - 1)
+    for ahead in range(1, blocks):
+        each(0, groups, lambda step: right_copy(ahead, step).start())
+    each(1, groups, lambda step: right_copy(0, step).start())
+    factor(w_left_gate, w_left, left)
+    each(1, groups, lambda step: left_copy(step).start())
+
+    gate[...] = jax.nn.sigmoid(
+        jnp.dot(normed[...], w_out_gate[...], preferred_element_type=jnp.float32)
+    )
+    left_mat[...] = jnp.zeros_like(left_mat)
+    right_mat[...] = jnp.zeros_like(right_mat)
+    lane = lax.broadcasted_iota(jnp.int32, (GROUP, LANES), 1)
+
+    def spread(chunk, target, half, start):
+        parts = [
+            chunk[:, at : at + LANES].astype(jnp.float32) for at in range(0, pairs, LANES)
+        ]
+        for line in range(rows):
+            at, off = divmod(line * cols, LANES)
+            part = parts[at]
+            if off:
+                part = pltpu.roll(part, LANES - off, 1)
+                if off + cols > LANES:
+                    part = jnp.where(
+                        lane < LANES - off, part, pltpu.roll(parts[at + 1], LANES - off, 1)
+                    )
+            part = jnp.where(lane < cols, part, 0.0)
+            target[half, pl.ds(pl.multiple_of((start + line) * GROUP, GROUP), GROUP), :] = part
+
+    def place_right(source, chunk):
+        line = source // col_size * rows
+        start = line // cols * LANES + line % cols
+        spread(chunk, right_mat, source % col_size, start)
+
+    def place_left(source, chunk):
+        spread(chunk, left_mat, source % col_size, source // col_size * rows)
+
+    place_right(flat, right[member])
+    place_left(member, left[member])
+
+    def take_right(ahead, step):
+        right_copy(ahead, step).wait_recv()
+        source = (block - ahead + blocks) % blocks * groups + (member - step + groups) % groups
+        place_right(source, right_all[source])
+
+    def take_left(step):
+        left_copy(step).wait_recv()
+        source = (member - step + groups) % groups
+        place_left(source, left_all[source])
+
+    each(1, groups, lambda step: take_right(0, step))
+    each(1, groups, take_left)
+    for ahead in range(1, blocks):
+        each(0, groups, lambda step: take_right(ahead, step))
+
+    block_lines = block_rows * rows
+
+    def channel(target, index, count):
+        return jnp.concatenate(
+            [
+                target[half, pl.ds(index, count, stride=GROUP), :].astype(jnp.bfloat16)
+                for half in range(col_size)
+            ],
+            axis=1,
+        )
+
+    for index in range(GROUP):
+        made = lax.dot_general(
+            channel(left_mat, index, block_lines),
+            channel(right_mat, index, col_size * LANES),
+            (((1,), (1,)), ((), ())),
+            preferred_element_type=jnp.float32,
+        )
+        for half in range(col_size):
+            product[half, pl.ds(index, block_lines, stride=GROUP), :] = made[
+                :, half * LANES : (half + 1) * LANES
+            ]
+
+    def pack(to):
+        half = to % col_size
+        start = to // col_size * rows
+        lines = [
+            product[half, pl.ds(pl.multiple_of((start + line) * GROUP, GROUP), GROUP), :]
+            for line in range(rows)
+        ]
+        for at in range(pairs // LANES):
+            low = at * LANES
+            line, off = divmod(low, cols)
+            part = pltpu.roll(lines[line], LANES - off, 1) if off else lines[line]
+            have = cols - off
+            while have < LANES:
+                line += 1
+                following = pltpu.roll(lines[line], have, 1)
+                part = jnp.where(lane < have, part, following)
+                have += cols
+            triangle[to, :, low : low + LANES] = part.astype(jnp.bfloat16)
+
+    each(0, groups, pack)
+    each(1, groups, lambda step: back_copy(step).start())
+    owned[member] = triangle[member]
+    each(1, groups, lambda step: left_copy(step).wait_send())
+    each(1, groups, lambda step: right_copy(0, step).wait_send())
+    for ahead in range(1, blocks):
+        each(0, groups, lambda step: right_copy(ahead, step).wait_send())
+    each(1, groups, lambda step: back_copy(step).wait())
+
+    for at in range(0, pairs, LANES):
+        piece = jnp.concatenate(
+            [owned[group, :, at : at + LANES].astype(jnp.float32) for group in range(groups)],
+            axis=0,
+        )
+        scaled = norm_axis(piece, 0).T.astype(jnp.bfloat16)
+        projected = jnp.dot(scaled, w_out[...], preferred_element_type=jnp.float32)
+        out[at : at + LANES] = (gate[at : at + LANES] * projected).astype(jnp.bfloat16)
+
+
+def fused(sizes, pair_act, tile_mask, *weights):
+    row_size, col_size, groups = sizes
+    devices = row_size * col_size
+    block_rows = groups // col_size
+    rows, cols, width = pair_act.shape
+    pairs = rows * cols
+    kept = pl.BlockSpec(memory_space=pltpu.VMEM)
+    dma = pltpu.SemaphoreType.DMA
+    chunks = pltpu.VMEM((groups, GROUP, pairs), jnp.bfloat16)
+    result = pl.pallas_call(
+        functools.partial(fused_kernel, sizes, pair_act.shape),
+        out_shape=jax.ShapeDtypeStruct((pairs, width), jnp.bfloat16),
+        in_specs=[kept] * 8,
+        out_specs=kept,
+        scratch_shapes=[
+            pltpu.VMEM((pairs, width), jnp.bfloat16),
+            pltpu.VMEM((pairs, width), jnp.float32),
+            chunks,
+            chunks,
+            chunks,
+            pltpu.VMEM((devices, GROUP, pairs), jnp.bfloat16),
+            pltpu.VMEM((col_size, block_rows * rows * GROUP, LANES), jnp.float32),
+            pltpu.VMEM((col_size, col_size * LANES * GROUP, LANES), jnp.float32),
+            pltpu.VMEM((col_size, block_rows * rows * GROUP, LANES), jnp.float32),
+            chunks,
+            chunks,
+            dma((groups,)),
+            dma((groups,)),
+            dma((devices,)),
+            dma((devices,)),
+            dma((groups,)),
+            dma((groups,)),
+        ],
+        compiler_params=pltpu.CompilerParams(collective_id=2, has_side_effects=True),
+    )(pair_act.reshape(pairs, width), tile_mask, *weights)
+    return result.reshape(rows, cols, width)
+
+
+def fits(sizes, rows, cols):
+    row_size, col_size, groups = sizes
+    pairs = rows * cols
+    return cols <= LANES and pairs % LANES == 0 and cols % rows == 0 and groups % col_size == 0
+
+
 def solution(mesh):
     def whole(pair_act, tile_mask, *weights):
         groups = pair_act.shape[2] // GROUP
         sizes = (mesh.shape["row"], mesh.shape["col"], groups)
+        rows, cols = (pair_act.shape[0] // sizes[0], pair_act.shape[1] // sizes[1])
+        body = fused if fits(sizes, rows, cols) else local
         return jax.shard_map(
-            functools.partial(local, sizes),
+            functools.partial(body, sizes),
             mesh=mesh,
             in_specs=(P("row", "col", None), P(), P(), P(), P(), P(), P(), P()),
             out_specs=P("row", "col", None),

time: 50.3 us -> 35 us (0.70)
  local copies, waits for them, and re-layouts: 11.8 us -> 1.69 us
  other arithmetic: 3.26 us -> 0 us
  matrix products: 3.08 us -> 0 us
  Pallas kernels: 31.5 us -> 33.1 us
    reshape x7 -> x0, local copies, waits for them, and re-layouts: 5.18 us -> none  [the longest x1 2.43 us: local(): right_all.reshape(row_size, col_size, GROUP, rows, cols)]
    dot_general x8 -> x0, matrix products: 3.08 us -> none  [the longest x4 1.1 us: project(): jnp.einsum('pd,de->ep', flat_normed, weight, preferred_element_type=jnp.f...]
    reduce_sum x4 -> x0, other arithmetic: 2.84 us -> none  [the longest x2 2.29 us: norm_axis(): mean = jnp.mean(values, axis=axis, keepdims=True)]
    convert_element_type x2 -> x0, local copies, waits for them, and re-layouts: 1.79 us -> none  [factor(): return out.astype(jnp.bfloat16).reshape(groups, GROUP, pairs)]
    pallas_call x2 -> x1, Pallas kernels: 31.5 us -> 33.1 us  [fused(): pl.pallas_call(functools.partial(fused_kernel, sizes, pair_act.shape), ou...]
    transpose x2 -> x0, local copies, waits for them, and re-layouts: 1.62 us -> none  [the longest x1 1.22 us: local(): right_rows = right_all.reshape(row_size, col_size, GROUP, rows, cols).tra...]
    unnamed x20 -> x1, local copies, waits for them, and re-layouts: 3.09 us -> 1.69 us
where the time goes in v2:
time: 35 us; the launch traced here: 34.8 us
  Pallas kernels  33.1 us (95%)
  local copies, waits for them, and re-layouts  1.69 us (5%)
    pallas_call x1, Pallas kernels, fused(): pl.pallas_call(functools.partial(fused_kernel, sizes, pair_act.shape), ou...  33.1 us
    unnamed x1, local copies, waits for them, and re-layouts  1.69 us

profile of v2, /device:TPU:0, one launch (start us, length us, event | category | flops | bytes accessed | tf_op | source)
XLA Modules:
  0.0 34.8 jit_solution(2757098624311937873)
XLA Ops:
  0.0 33.1 %shard_map.82 = bf16[1152,128]{1,0:T(8,128)(2,1)} custom-call(bf16[1152,128]{1,0:T(8,128)(2,1)} %bitcast.3, s32[12,12]{1,0:T(8,128)} %tiles.1, bf16[128,128]{1,0:T(8,128)(2,1)} %w_left_gate.1, bf16[128,128]{1,0:T(8,128)(2,1)} %w_left.1, bf16[128,128]{1,0:T(8,128)(2,1)} %w_right_gate.1, bf16[128,128]{1,0:T(8,128)(2,1)} %w_right.1, ...), custom_call_target="tpu_custom_call" | custom-call | tf_op jit(solution)/shard_map/pallas_call | solution.py:444
  33.2 1.7 %copy.10 = bf16[12,96,128]{2,1,0:T(8,128)(2,1)} copy(bf16[12,96,128]{2,1,0:T(8,128)(2,1)} %bitcast.2) | data formatting | bytes 589824

commit v3 on v2

--- a/solution.py
+++ b/solution.py
@@ -226,10 +226,19 @@
 
 
 def fused_kernel(
-    sizes, shape, pair, tiles, w_left_gate, w_left, w_right_gate, w_right, w_out_gate, w_out, out,
-    normed, gate, left, right, left_all, right_all, left_mat, right_mat, product, triangle, owned,
-    left_send, left_recv, right_send, right_recv, back_send, back_recv,
+    sizes, shape, pair_in, tiles_in, *rest
 ):
+    weights_in, out = rest[:6], rest[6]
+    (
+        pair, tiles, w_left_gate, w_left, w_right_gate, w_right, w_out_gate, w_out, input_sem,
+        normed, gate, left, right, left_all, right_all, left_mat, right_mat, left_lines, product, triangle, owned,
+        left_send, left_recv, right_send, right_recv, back_send, back_recv,
+    ) = rest[7:]
+    kept = (pair, tiles, w_left_gate, w_left, w_right_gate, w_right, w_out_gate, w_out)
+    fetches = [
+        pltpu.make_async_copy(source, target, input_sem.at[index])
+        for index, (source, target) in enumerate(zip((pair_in, tiles_in, *weights_in), kept))
+    ]
     row_size, col_size, groups = sizes
     rows, cols, width = shape
     devices = row_size * col_size
@@ -251,11 +260,17 @@
         )
         return 0
 
+    fetches[0].start()
     lax.fori_loop(1, devices, signal, 0)
+    for fetch in fetches[1:]:
+        fetch.start()
+    fetches[0].wait()
 
     values = pair[...].astype(jnp.float32)
     normed[...] = norm_axis(values, 1).astype(jnp.bfloat16)
 
+    for fetch in fetches[1:]:
+        fetch.wait()
     spot = lax.broadcasted_iota(jnp.int32, (1, pairs), 1)
     within = spot
     for line in range(1, rows):
@@ -304,8 +319,15 @@
     def left_copy(step):
         return member_copy(left, left_all, left_send, left_recv, step)
 
-    def back_copy(step):
-        return member_copy(triangle, owned, back_send, back_recv, step)
+    def back_copy(to, slot):
+        return pltpu.make_async_remote_copy(
+            src_ref=triangle.at[to],
+            dst_ref=owned.at[slot],
+            send_sem=back_send.at[to],
+            recv_sem=back_recv.at[slot],
+            device_id=place(first + to, col_size),
+            device_id_type=MESH,
+        )
 
     def each(start, stop, do):
         def body(step, _):
@@ -315,12 +337,12 @@
         lax.fori_loop(start, stop, body, 0)
 
     factor(w_right_gate, w_right, right)
+    factor(w_left_gate, w_left, left)
     pl.semaphore_wait(barrier, devices - 1)
+    each(1, groups, lambda step: right_copy(0, step).start())
+    each(1, groups, lambda step: left_copy(step).start())
     for ahead in range(1, blocks):
         each(0, groups, lambda step: right_copy(ahead, step).start())
-    each(1, groups, lambda step: right_copy(0, step).start())
-    factor(w_left_gate, w_left, left)
-    each(1, groups, lambda step: left_copy(step).start())
 
     gate[...] = jax.nn.sigmoid(
         jnp.dot(normed[...], w_out_gate[...], preferred_element_type=jnp.float32)
@@ -368,59 +390,70 @@
 
     each(1, groups, lambda step: take_right(0, step))
     each(1, groups, take_left)
-    for ahead in range(1, blocks):
-        each(0, groups, lambda step: take_right(ahead, step))
-
     block_lines = block_rows * rows
 
-    def channel(target, index, count):
+    def channel(target, index, start, count):
+        first_line = pl.multiple_of(start * GROUP, GROUP) + index
         return jnp.concatenate(
             [
-                target[half, pl.ds(index, count, stride=GROUP), :].astype(jnp.bfloat16)
+                target[half, pl.ds(first_line, count, stride=GROUP), :].astype(jnp.bfloat16)
                 for half in range(col_size)
             ],
             axis=1,
         )
 
     for index in range(GROUP):
-        made = lax.dot_general(
-            channel(left_mat, index, block_lines),
-            channel(right_mat, index, col_size * LANES),
-            (((1,), (1,)), ((), ())),
-            preferred_element_type=jnp.float32,
-        )
-        for half in range(col_size):
-            product[half, pl.ds(index, block_lines, stride=GROUP), :] = made[
-                :, half * LANES : (half + 1) * LANES
+        left_lines[index] = channel(left_mat, index, 0, block_lines)
+
+    def finish(half):
+        for index in range(GROUP):
+            made = lax.dot_general(
+                left_lines[index],
+                channel(right_mat, index, half * LANES, LANES),
+                (((1,), (1,)), ((), ())),
+                preferred_element_type=jnp.float32,
+            )
+            product[pl.ds(index, block_lines, stride=GROUP), :] = made
+
+        def pack(step):
+            part_row = (member // col_size + step) % block_rows
+            to = part_row * col_size + half
+            lines = [
+                product[pl.ds(pl.multiple_of((part_row * rows + line) * GROUP, GROUP), GROUP), :]
+                for line in range(rows)
             ]
-
-    def pack(to):
-        half = to % col_size
-        start = to // col_size * rows
-        lines = [
-            product[half, pl.ds(pl.multiple_of((start + line) * GROUP, GROUP), GROUP), :]
-            for line in range(rows)
-        ]
-        for at in range(pairs // LANES):
-            low = at * LANES
-            line, off = divmod(low, cols)
-            part = pltpu.roll(lines[line], LANES - off, 1) if off else lines[line]
-            have = cols - off
-            while have < LANES:
-                line += 1
-                following = pltpu.roll(lines[line], have, 1)
-                part = jnp.where(lane < have, part, following)
-                have += cols
-            triangle[to, :, low : low + LANES] = part.astype(jnp.bfloat16)
-
-    each(0, groups, pack)
-    each(1, groups, lambda step: back_copy(step).start())
+            for at in range(pairs // LANES):
+                low = at * LANES
+                line, off = divmod(low, cols)
+                part = pltpu.roll(lines[line], LANES - off, 1) if off else lines[line]
+                have = cols - off
+                while have < LANES:
+                    line += 1
+                    part = jnp.where(lane < have, part, pltpu.roll(lines[line], have, 1))
+                    have += cols
+                triangle[to, :, low : low + LANES] = part.astype(jnp.bfloat16)
+
+            @pl.when(to != member)
+            def _():
+                back_copy(to, member).start()
+
+        each(0, block_rows, pack)
+
+    finish(block)
+    for ahead in range(1, blocks):
+        each(0, groups, lambda step: take_right(ahead, step))
+        finish((block - ahead + blocks) % blocks)
     owned[member] = triangle[member]
     each(1, groups, lambda step: left_copy(step).wait_send())
     each(1, groups, lambda step: right_copy(0, step).wait_send())
     for ahead in range(1, blocks):
         each(0, groups, lambda step: right_copy(ahead, step).wait_send())
-    each(1, groups, lambda step: back_copy(step).wait())
+
+    def wait_back(step):
+        other = (member + step) % groups
+        back_copy(other, other).wait()
+
+    each(1, groups, wait_back)
 
     for at in range(0, pairs, LANES):
         piece = jnp.concatenate(
@@ -444,9 +477,13 @@
     result = pl.pallas_call(
         functools.partial(fused_kernel, sizes, pair_act.shape),
         out_shape=jax.ShapeDtypeStruct((pairs, width), jnp.bfloat16),
-        in_specs=[kept] * 8,
+        in_specs=[pl.BlockSpec(memory_space=pltpu.HBM)] * 8,
         out_specs=kept,
         scratch_shapes=[
+            pltpu.VMEM((pairs, width), jnp.bfloat16),
+            pltpu.VMEM(tile_mask.shape, tile_mask.dtype),
+            *[pltpu.VMEM(weight.shape, weight.dtype) for weight in weights],
+            dma((8,)),
             pltpu.VMEM((pairs, width), jnp.bfloat16),
             pltpu.VMEM((pairs, width), jnp.float32),
             chunks,
@@ -455,7 +492,8 @@
             pltpu.VMEM((devices, GROUP, pairs), jnp.bfloat16),
             pltpu.VMEM((col_size, block_rows * rows * GROUP, LANES), jnp.float32),
             pltpu.VMEM((col_size, col_size * LANES * GROUP, LANES), jnp.float32),
-            pltpu.VMEM((col_size, block_rows * rows * GROUP, LANES), jnp.float32),
+            pltpu.VMEM((GROUP, block_rows * rows, col_size * LANES), jnp.bfloat16),
+            pltpu.VMEM((block_rows * rows * GROUP, LANES), jnp.float32),
             chunks,
             chunks,
             dma((groups,)),
@@ -473,7 +511,9 @@
 def fits(sizes, rows, cols):
     row_size, col_size, groups = sizes
     pairs = rows * cols
-    return cols <= LANES and pairs % LANES == 0 and cols % rows == 0 and groups % col_size == 0
+    if row_size * col_size != groups * col_size or groups % col_size:
+        return False
+    return cols <= LANES and pairs % LANES == 0 and cols % rows == 0
 
 
 def solution(mesh):

time: 35 us -> 30.5 us (0.87)
  Pallas kernels: 33.1 us -> 28.3 us
    pallas_call x1, Pallas kernels: 33.1 us -> 28.3 us  [fused(): pl.pallas_call(functools.partial(fused_kernel, sizes, pair_act.shape), ou...]
where the time goes in v3:
time: 30.5 us; the launch traced here: 30 us
  Pallas kernels  28.3 us (93%)
  local copies, waits for them, and re-layouts  1.69 us (6%)
    pallas_call x1, Pallas kernels, fused(): pl.pallas_call(functools.partial(fused_kernel, sizes, pair_act.shape), ou...  28.3 us
    unnamed x1, local copies, waits for them, and re-layouts  1.69 us

profile of v3, /device:TPU:0, one launch (start us, length us, event | category | flops | bytes accessed | tf_op | source)
XLA Modules:
  0.0 30.0 jit_solution(348657904963524090)
XLA Ops:
  0.0 28.3 %shard_map.82 = bf16[1152,128]{1,0:T(8,128)(2,1)} custom-call(bf16[1152,128]{1,0:T(8,128)(2,1)} %bitcast.3, s32[12,12]{1,0:T(8,128)} %tiles_in.1, bf16[128,128]{1,0:T(8,128)(2,1)} %rest_0_.1, bf16[128,128]{1,0:T(8,128)(2,1)} %rest_1_.1, bf16[128,128]{1,0:T(8,128)(2,1)} %rest_2_.1, bf16[128,128]{1,0:T(8,128)(2,1)} %rest_3_.1, bf16[128,128]{1,0:T(8,128)(2,1)} %rest_4_.1, ...), custom_call_target="tpu_custom_call" | custom-call | tf_op jit(solution)/shard_map/pallas_call | solution.py:477
  28.3 1.7 %copy.10 = bf16[12,96,128]{2,1,0:T(8,128)(2,1)} copy(bf16[12,96,128]{2,1,0:T(8,128)(2,1)} %bitcast.2) | data formatting | bytes 589824

commit v4 on v3

--- a/solution.py
+++ b/solution.py
@@ -230,7 +230,7 @@
 ):
     weights_in, out = rest[:6], rest[6]
     (
-        pair, tiles, w_left_gate, w_left, w_right_gate, w_right, w_out_gate, w_out, input_sem,
+        pair, tiles, w_left_gate, w_left, w_right_gate, w_right, w_out_gate, w_out, input_sem, made_out, out_sem,
         normed, gate, left, right, left_all, right_all, left_mat, right_mat, left_lines, product, triangle, owned,
         left_send, left_recv, right_send, right_recv, back_send, back_recv,
     ) = rest[7:]
@@ -455,6 +455,11 @@
 
     each(1, groups, wait_back)
 
+    def hand_out(at):
+        return pltpu.make_async_copy(
+            made_out.at[pl.ds(at, LANES)], out.at[pl.ds(at, LANES)], out_sem.at[at // LANES]
+        )
+
     for at in range(0, pairs, LANES):
         piece = jnp.concatenate(
             [owned[group, :, at : at + LANES].astype(jnp.float32) for group in range(groups)],
@@ -462,7 +467,10 @@
         )
         scaled = norm_axis(piece, 0).T.astype(jnp.bfloat16)
         projected = jnp.dot(scaled, w_out[...], preferred_element_type=jnp.float32)
-        out[at : at + LANES] = (gate[at : at + LANES] * projected).astype(jnp.bfloat16)
+        made_out[at : at + LANES] = (gate[at : at + LANES] * projected).astype(jnp.bfloat16)
+        hand_out(at).start()
+    for at in range(0, pairs, LANES):
+        hand_out(at).wait()
 
 
 def fused(sizes, pair_act, tile_mask, *weights):
@@ -478,12 +486,14 @@
         functools.partial(fused_kernel, sizes, pair_act.shape),
         out_shape=jax.ShapeDtypeStruct((pairs, width), jnp.bfloat16),
         in_specs=[pl.BlockSpec(memory_space=pltpu.HBM)] * 8,
-        out_specs=kept,
+        out_specs=pl.BlockSpec(memory_space=pltpu.HBM),
         scratch_shapes=[
             pltpu.VMEM((pairs, width), jnp.bfloat16),
             pltpu.VMEM(tile_mask.shape, tile_mask.dtype),
             *[pltpu.VMEM(weight.shape, weight.dtype) for weight in weights],
             dma((8,)),
+            pltpu.VMEM((pairs, width), jnp.bfloat16),
+            dma((pairs // LANES,)),
             pltpu.VMEM((pairs, width), jnp.bfloat16),
             pltpu.VMEM((pairs, width), jnp.float32),
             chunks,

time: 30.5 us -> 30.5 us (level)
  no operation moved by 1% of the time
where the time goes in v4:
time: 30.5 us; the launch traced here: 30 us
  Pallas kernels  28.3 us (93%)
  local copies, waits for them, and re-layouts  1.69 us (6%)
    pallas_call x1, Pallas kernels, fused(): pl.pallas_call(functools.partial(fused_kernel, sizes, pair_act.shape), ou...  28.3 us
    unnamed x1, local copies, waits for them, and re-layouts  1.69 us

profile of v4, /device:TPU:0, one launch (start us, length us, event | category | flops | bytes accessed | tf_op | source)
XLA Modules:
  0.0 30.0 jit_solution(2457470791879246828)
XLA Ops:
  0.0 28.3 %shard_map.82 = bf16[1152,128]{1,0:T(8,128)(2,1)} custom-call(bf16[1152,128]{1,0:T(8,128)(2,1)} %bitcast.3, s32[12,12]{1,0:T(8,128)} %tiles_in.1, bf16[128,128]{1,0:T(8,128)(2,1)} %rest_0_.1, bf16[128,128]{1,0:T(8,128)(2,1)} %rest_1_.1, bf16[128,128]{1,0:T(8,128)(2,1)} %rest_2_.1, bf16[128,128]{1,0:T(8,128)(2,1)} %rest_3_.1, bf16[128,128]{1,0:T(8,128)(2,1)} %rest_4_.1, ...), custom_call_target="tpu_custom_call" | custom-call | tf_op jit(solution)/shard_map/pallas_call | solution.py:485
  28.3 1.7 %copy.10 = bf16[12,96,128]{2,1,0:T(8,128)(2,1)} copy(bf16[12,96,128]{2,1,0:T(8,128)(2,1)} %bitcast.2) | data formatting | bytes 589824
